TPU v7x, 256 devices: a whole 4x4x8 slice. The times are simulated.
256 devices in a mesh: wide: 32 (over z_hi, y, core), shard: 8 (over z_lo, x).
Axes of the slice: x: 4, y: 4, z: 8 (z_hi: 4, z_lo: 2; z = z_hi * 2 + z_lo), core: 2. Of those that a mesh axis runs over, the one named last changes fastest.
Arguments:
- weights: bfloat16 [1024, 8192], P('shard'), may hold values from -6 to 6
- momentum: bfloat16 [32, 1024, 8192], P('wide', 'shard'), may hold values from -6 to 6
- grads: bfloat16 [2, 32, 1024, 8192], P(None, 'wide', 'shard'), may hold values from -6 to 6
- offsets: int32 [8, 64], P('shard'), may hold values from 0 to 96
- owners: int32 [8, 64], P('shard'), may hold values from 0 to 63, each once within a row
- exp_avg: float32 [8, 64, 32, 128], P('shard', 'wide'), may hold values from -7 to 7
- exp_sq: float32 [8, 64, 32, 128], P('shard', 'wide'), may hold values from 0.01 to 1
Outputs:
- new_weights: bfloat16 [1024, 8192], P('shard')
- new_momentum: bfloat16 [32, 1024, 8192], P('wide', 'shard')
- new_avg: float32 [8, 64, 32, 128], P('shard', 'wide')
- new_sq: float32 [8, 64, 32, 128], P('shard', 'wide')
- scales: float32 [2], replicated
Inputs may be any that keep to these rules, and one draw needn't show every extreme that they name: `offsets`: each block's band spans 32 consecutive transform rows. Each row of owners is a permutation of 0 to 63.
All inputs are finite; a program needn't handle non-finite values.
Results may differ from a plain program's by a relative error of at most 0.003.
Values may be sent and summed in bfloat16 or wider, within the bound.
A program may use at most 128 MiB of HBM per device.

v0:
```python
import functools

import jax
import jax.numpy as jnp
from jax import lax
from jax.sharding import Mesh
from jax.sharding import PartitionSpec as P

STEPS = 2
WIDE = ("wide_0", "wide_1", "wide_2")
SHARD = ("shard_0", "shard_1")
WIDE_SHARD = ("wide_0", "wide_1", "wide_2", "shard_0", "shard_1")


highest = lax.Precision.HIGHEST
momentum_decay = 0.9
beta_one = 0.8
beta_two = 0.95
adam_eps = 1e-08
rms_eps = 1e-06
learning_rate = 0.2


def one_axis_at_a_time(shard, axes):
    return functools.reduce(lax.psum, axes, shard)


def laid_out(parts, dim):
    parts = jnp.moveaxis(parts, 0, dim)
    lengths = parts.shape
    return parts.reshape(*lengths[:dim], lengths[dim] * lengths[dim + 1], *lengths[dim + 2 :])


def from_everyone(shard, axis):
    length = lax.axis_size(axis)
    return lax.all_to_all(
        jnp.broadcast_to(shard[None], (length, *shard.shape)), axis, 0, 0, tiled=True
    )


def gathered_copies(shard, axis, dim):
    return laid_out(from_everyone(shard, axis), dim)


def dct_table(length):
    frequency = jnp.arange(length, dtype=jnp.float32)[:, None]
    position = jnp.arange(length, dtype=jnp.float32)[None, :]
    cosines = jnp.cos(jnp.pi * (2.0 * position + 1.0) * frequency / (2.0 * length))
    scaling = jnp.where(frequency == 0.0, jnp.sqrt(1.0 / length), jnp.sqrt(2.0 / length))
    return cosines * scaling


def band_tables(basis, offsets, band_rows):
    indices = offsets[:, :, None] + jnp.arange(band_rows, dtype=jnp.int32)[None, None, :]
    return basis[indices]


def inverse(coefs, picked, basis):
    right_part = jnp.einsum("rjpc,cb->rjpb", coefs, basis, precision=highest)
    return jnp.einsum("rjpa,rjpb->rajb", picked, right_part, precision=highest)


def per_device(weights, momentum, grads, offsets, owners, exp_avg, exp_sq):
    block_len = exp_avg.shape[3]
    band_rows = exp_avg.shape[2]
    basis = dct_table(block_len)
    picked = band_tables(basis, offsets, band_rows)
    slot_order = jnp.argsort(owners, axis=1)
    row_blocks = offsets.shape[0]
    col_blocks = offsets.shape[1]
    block_shape = (row_blocks, block_len, col_blocks, block_len)
    replicas = lax.axis_size(WIDE)
    count_all = exp_avg.size * lax.axis_size(WIDE) * lax.axis_size(SHARD)
    weight_now = weights.astype(jnp.float32).reshape(block_shape)
    moment_now = momentum[0].astype(jnp.float32).reshape(block_shape)
    avg_now = exp_avg
    sq_now = exp_sq
    scales = []
    for step_index in range(STEPS):
        blended = momentum_decay * moment_now + grads[step_index, 0].astype(jnp.float32).reshape(
            block_shape
        )
        left_part = jnp.einsum("rjpa,rajb->rjpb", picked, blended, precision=highest)
        band_coef = jnp.einsum("rjpb,cb->rjpc", left_part, basis, precision=highest)
        moment_now = blended - inverse(band_coef, picked, basis)
        slot_band = jnp.take_along_axis(band_coef, slot_order[:, :, None, None], axis=1)
        pieces = lax.all_to_all(
            slot_band.astype(jnp.bfloat16), WIDE, split_axis=1, concat_axis=0, tiled=True
        ).astype(slot_band.dtype)
        summed = jnp.sum(pieces.reshape((replicas, row_blocks) + pieces.shape[1:]), axis=0)
        mean_band = summed / replicas
        avg_now = beta_one * avg_now + (1.0 - beta_one) * mean_band
        sq_now = beta_two * sq_now + (1.0 - beta_two) * mean_band * mean_band
        raw_update = avg_now / (jnp.sqrt(sq_now) + adam_eps)
        power_sum = one_axis_at_a_time(jnp.sum(raw_update * raw_update), WIDE_SHARD)
        spread = jnp.sqrt(power_sum / count_all + rms_eps)
        update = (raw_update / spread).astype(jnp.bfloat16)
        gathered = gathered_copies(update, WIDE, 1)
        block_update = jnp.take_along_axis(
            gathered.astype(jnp.float32), owners[:, :, None, None], axis=1
        )
        weight_now = weight_now - learning_rate * inverse(block_update, picked, basis)
        scales.append(spread)
    new_weights = weight_now.reshape(weights.shape).astype(jnp.bfloat16)
    new_momentum = moment_now.reshape(momentum.shape).astype(jnp.bfloat16)
    return (new_weights, new_momentum, avg_now, sq_now, jnp.stack(scales))


def solution(mesh):
    split = Mesh(
        mesh.devices.reshape(4, 4, 2, 2, 4), ("wide_0", "wide_1", "wide_2", "shard_0", "shard_1")
    )
    in_specs = (
        P(SHARD, None),
        P(WIDE, SHARD, None),
        P(None, WIDE, SHARD, None),
        P(SHARD, None),
        P(SHARD, None),
        P(SHARD, WIDE, None, None),
        P(SHARD, WIDE, None, None),
    )
    out_specs = (
        P(SHARD, None),
        P(WIDE, SHARD, None),
        P(SHARD, WIDE, None, None),
        P(SHARD, WIDE, None, None),
        P(),
    )
    return jax.shard_map(
        per_device, mesh=split, in_specs=in_specs, out_specs=out_specs, check_vma=False
    )
```

profile of v0, /device:TPU:1, one launch (start us, length us, event | category | flops | bytes accessed | tf_op | source)
XLA Modules:
  0.0 243.2 jit_solution(2718648643845490075)
XLA Ops:
  3.4 6.6 %slice_convert_fusion.1 = (f32[1,1,128,8192]{3,2,1,0:T(8,128)}, f32[16,8,64,128]{3,1,2,0:T(8,128)S(1)}, f32[1,1,128,8192]{3,2,1,0:T(8,128)}) fusion(bf16[2,1,128,8192]{3,2,1,0:T(8,128)(2,1)} %param.11), kind=kLoop, calls=%fused_computation.20 | loop fusion | flops 2097152 | bytes 16777216 | tf_op jit(solution)/shard_map/convert_element_type | solution.py:80
  18.2 5.7 %gather_fusion = f32[2048,128]{1,0:T(8,128)S(1)} fusion(f32[128,128]{1,0:T(8,128)S(1)} %cosine_multiply_fusion, s32[2048]{0:T(1024)S(1)} %broadcast_clamp_fusion), kind=kCustom, calls=%fused_computation.4 | custom fusion | bytes 2105344 | tf_op jit(solution)/shard_map/gather | solution.py:55
  23.9 12.7 %fusion.6 = f32[64,32,128]{2,1,0:T(8,128)S(1)} fusion(f32[64,32,128]{2,1,0:T(8,128)S(1)} %bitcast.181, f32[128,64,128]{2,1,0:T(8,128)} %bitcast.188, f32[128,64,128]{2,1,0:T(8,128)} %bitcast.189), kind=kOutput, calls=%fused_computation.16 | convolution fusion | flops 403701760 | bytes 10485760 | tf_op jit(solution)/shard_map/rjpa,rajb->rjpb/dot_general | solution.py:83
  39.0 5.6 %copy.41 = f32[1,1,128,8192]{2,3,1,0:T(8,128)} copy(f32[1,1,128,8192]{3,2,1,0:T(8,128)} %get-tuple-element.41) | data formatting | bytes 8388608 | tf_op jit(solution)/shard_map/convert_element_type | solution.py:80
  44.6 5.6 %copy.42 = f32[1,1,128,8192]{2,3,1,0:T(8,128)} copy(f32[1,1,128,8192]{3,2,1,0:T(8,128)} %get-tuple-element.43) | data formatting | bytes 8388608 | tf_op jit(solution)/shard_map/convert_element_type | solution.py:80
  50.2 5.6 %copy.40 = f32[1,128,8192]{1,2,0:T(8,128)} copy(f32[1,128,8192]{2,1,0:T(8,128)} %get-tuple-element.44) | data formatting | bytes 8388608 | tf_op jit(solution)/shard_map/mul | solution.py:80
  55.7 10.4 %fusion.3 = f32[1,128,64,128]{1,3,2,0:T(8,128)S(1)} fusion(f32[1,128,64,128]{1,3,2,0:T(8,128)} %bitcast.191, f32[1,128,64,128]{1,3,2,0:T(8,128)} %bitcast.192, f32[1,128,64,128]{1,3,2,0:T(8,128)} %bitcast.190, f32[64,32,128]{2,1,0:T(8,128)S(1)} %fusion.27, f32[64,32,128]{2,1,0:T(8,128)S(1)} %bitcast.182), kind=kOutput, calls=%fused_computation.11 | convolution fusion | flops 406847488 | bytes 18874368 | tf_op jit(solution)/shard_map/rjpa,rjpb->rajb/dot_general | solution.py:60
  66.2 6.7 %fusion.4 = f32[64,32,128]{2,1,0:T(8,128)S(1)} fusion(f32[64,32,128]{2,1,0:T(8,128)S(1)} %bitcast.183, f32[1,128,64,128]{1,3,2,0:T(8,128)S(1)} %fusion.3), kind=kOutput, calls=%fused_computation.13 | convolution fusion | flops 402653184 | bytes 6291456 | tf_op jit(solution)/shard_map/rjpa,rajb->rjpb/dot_general | solution.py:83
  78.3 30.7 %all_to_all.28 = bf16[1,64,32,128]{3,2,0,1:T(8,128)(2,1)S(1)} all-to-all(bf16[1,64,32,128]{3,2,0,1:T(8,128)(2,1)S(1)} %get-tuple-element.47), channel_id=1, replica_groups=mesh['wide_0'=4,'wide_1'=4,'wide_2'=2,'shard_0'=2,'shard_1'=4] {'wide_0'..., dimensions={1} | all-to-all | bytes 1048576 | tf_op jit(solution)/shard_map/all_to_all | solution.py:87
  109.0 4.2 %all-to-all-start = ((bf16[1,64,32,128]{3,2,0,1:T(8,128)(2,1)}), bf16[1,64,32,128]{3,2,0,1:T(8,128)(2,1)S(1)}, u32[]{:S(2)}, u32[]{:S(2)}) async-start(bf16[1,64,32,128]{3,2,0,1:T(8,128)(2,1)} %get-tuple-element.48), calls=%async_computation | async-start | bytes 1048576 | tf_op jit(solution)/shard_map/all_to_all | solution.py:87
  113.3 17.1 %all-to-all-done = bf16[1,64,32,128]{3,2,0,1:T(8,128)(2,1)S(1)} async-done(((bf16[1,64,32,128]{3,2,0,1:T(8,128)(2,1)}), bf16[1,64,32,128]{3,2,0,1:T(8,128)(2,1)S(1)}, u32[]{:S(2)}, u32[]{:S(2)}) %all-to-all-start) | async-done | bytes 524320 | tf_op jit(solution)/shard_map/all_to_all | solution.py:87
  131.2 9.8 %all-reduce.2 = (f32[]{:T(128)}, f32[]{:T(128)}) all-reduce(f32[]{:T(128)} %get-tuple-element.46, f32[]{:T(128)} %get-tuple-element.38), channel_id=1, replica_groups=mesh['wide_0'=4,'wide_1'=4,'wide_2'=2,'shard_0'=2,'shard_1'=4] {'wide_0'}, use_global_device_ids=true, to_apply=%region_3.5 | all-reduce | flops 2 | bytes 16 | tf_op jit(solution)/shard_map/psum | solution.py:25
  141.0 7.8 %all-reduce.1 = (f32[]{:T(128)}, f32[]{:T(128)}) all-reduce(f32[]{:T(128)} %get-tuple-element.32, f32[]{:T(128)} %get-tuple-element.33), channel_id=1, replica_groups=mesh['wide_0'=4,'wide_1'=4,'wide_2'=2,'shard_0'=2,'shard_1'=4] {'wide_1'}, use_global_device_ids=true, to_apply=%region_4.6 | all-reduce | flops 2 | bytes 16 | tf_op jit(solution)/shard_map/psum | solution.py:25
  148.9 6.8 %all-reduce.4 = (f32[]{:T(128)}, f32[]{:T(128)}) all-reduce(f32[]{:T(128)} %get-tuple-element.30, f32[]{:T(128)} %get-tuple-element.31), channel_id=1, replica_groups=mesh['wide_0'=4,'wide_1'=4,'wide_2'=2,'shard_0'=2,'shard_1'=4] {'wide_2'}, use_global_device_ids=true, to_apply=%region_5.7 | all-reduce | flops 2 | bytes 16 | tf_op jit(solution)/shard_map/psum | solution.py:25
  155.6 4.4 %all-reduce.3 = (f32[]{:T(128)}, f32[]{:T(128)}) all-reduce(f32[]{:T(128)} %get-tuple-element.36, f32[]{:T(128)} %get-tuple-element.37), channel_id=1, replica_groups=mesh['wide_0'=4,'wide_1'=4,'wide_2'=2,'shard_0'=2,'shard_1'=4] {'shard_0'}, use_global_device_ids=true, to_apply=%region_6.8 | all-reduce | flops 2 | bytes 16 | tf_op jit(solution)/shard_map/psum | solution.py:25
  160.0 9.1 %all-reduce = (f32[]{:T(128)}, f32[]{:T(128)}) all-reduce(f32[]{:T(128)} %get-tuple-element.34, f32[]{:T(128)} %get-tuple-element.35), channel_id=1, replica_groups=mesh['wide_0'=4,'wide_1'=4,'wide_2'=2,'shard_0'=2,'shard_1'=4] {'shard_1'}, use_global_device_ids=true, to_apply=%region_7.9 | all-reduce | flops 2 | bytes 16 | tf_op jit(solution)/shard_map/psum | solution.py:25
  170.8 7.6 %all-to-all-start.3 = ((bf16[32,1,2,32,128]{4,3,2,1,0:T(8,128)(2,1)}), bf16[32,1,2,32,128]{4,3,2,1,0:T(8,128)(2,1)S(1)}, u32[]{:S(2)}, u32[]{:S(2)}) async-start(bf16[32,1,2,32,128]{4,3,2,1,0:T(8,128)(2,1)} %broadcast_in_dim.50), calls=%async_computation.3 | async-start | bytes 1048576 | tf_op jit(solution)/shard_map/all_to_all | solution.py:36
  181.3 14.0 %all-to-all-done.3 = bf16[32,1,2,32,128]{4,3,2,1,0:T(8,128)(2,1)S(1)} async-done(((bf16[32,1,2,32,128]{4,3,2,1,0:T(8,128)(2,1)}), bf16[32,1,2,32,128]{4,3,2,1,0:T(8,128)(2,1)S(1)}, u32[]{:S(2)}, u32[]{:S(2)}) %all-to-all-start.3) | async-done | bytes 524320 | tf_op jit(solution)/shard_map/all_to_all | solution.py:36
  196.2 5.8 %all-to-all-start.1 = ((bf16[32,1,2,32,128]{4,3,2,1,0:T(8,128)(2,1)}), bf16[32,1,2,32,128]{4,3,2,1,0:T(8,128)(2,1)}, u32[]{:S(2)}, u32[]{:S(2)}) async-start(bf16[32,1,2,32,128]{4,3,2,1,0:T(8,128)(2,1)} %broadcast_in_dim.47), calls=%async_computation.1 | async-start | bytes 1048576 | tf_op jit(solution)/shard_map/all_to_all | solution.py:36
  202.1 8.7 %fusion = bf16[1,128,64,128]{1,3,2,0:T(8,128)(2,1)S(1)} fusion(f32[1,128,64,128]{1,3,2,0:T(8,128)} %copy-done, f32[64,32,128]{2,1,0:T(8,128)} %fusion.22, f32[64,32,128]{2,1,0:T(8,128)S(1)} %bitcast.184), kind=kOutput, calls=%fused_computation.6 | convolution fusion | flops 404750336 | bytes 8388608 | tf_op jit(solution)/shard_map/rjpa,rjpb->rajb/dot_general | solution.py:60
  210.8 2.9 %copy.46 = bf16[1,128,8192]{2,1,0:T(8,128)(2,1)} copy(bf16[1,128,8192]{1,2,0:T(8,128)(2,1)S(1)} %bitcast.194) | data formatting | bytes 4194304
  213.7 4.3 %copy.35 = f32[128,8192]{0,1:T(8,128)} copy(bf16[128,8192]{1,0:T(8,128)(2,1)} %param.9) | data formatting | bytes 6291456 | tf_op jit(solution)/shard_map/reshape | solution.py:74
  226.0 6.7 %fusion.62 = f32[64,128,128]{2,1,0:T(8,128)S(1)} fusion(f32[64,32,128]{2,1,0:T(8,128)S(1)} %fusion.11, f32[64,32,128]{2,1,0:T(8,128)S(1)} %bitcast.185), kind=kOutput, calls=%fused_computation.105 | convolution fusion | flops 402653184 | bytes 6291456 | tf_op jit(solution)/shard_map/rjpa,rjpb->rajb/dot_general | solution.py:60
  232.8 7.3 %fusion.1 = bf16[1,128,64,128]{1,3,2,0:T(8,128)(2,1)S(1)} fusion(f32[1,128,64,128]{1,3,2,0:T(8,128)S(1)} %bitcast.187, f32[64,128,128]{2,1,0:T(8,128)S(1)} %fusion.62, f32[64,32,128]{2,1,0:T(8,128)S(1)} %fusion.8, f32[64,32,128]{2,1,0:T(8,128)S(1)} %bitcast.186), kind=kOutput, calls=%fused_computation.8 | convolution fusion | flops 407896064 | bytes 12582912 | tf_op jit(solution)/shard_map/rjpa,rjpb->rajb/dot_general | solution.py:60
  (61 shorter events, 34.6 us)
Async XLA Ops:
  10.0 2.7 %copy-start.2 = (bf16[1,128,8192]{2,1,0:T(8,128)(2,1)S(1)}, bf16[1,128,8192]{2,1,0:T(8,128)(2,1)}, u32[]{:S(2)}) copy-start(bf16[1,128,8192]{2,1,0:T(8,128)(2,1)} %param.10) | copy-start | bytes 6291460
  66.2 7.9 %copy-start = (f32[1,128,64,128]{1,3,2,0:T(8,128)}, f32[1,128,64,128]{1,3,2,0:T(8,128)S(1)}, u32[]{:S(2)}) copy-start(f32[1,128,64,128]{1,3,2,0:T(8,128)S(1)} %fusion.3) | copy-start | bytes 12582916
  74.1 56.5 %copy-start.5 = (f32[1,2,32,128]{3,2,1,0:T(8,128)S(1)}, f32[1,2,32,128]{3,2,1,0:T(8,128)}, u32[]{:S(2)}) copy-start(f32[1,2,32,128]{3,2,1,0:T(8,128)} %param.15) | copy-start | bytes 98308
  74.1 56.5 %copy-start.6 = (f32[1,2,32,128]{3,2,1,0:T(8,128)S(1)}, f32[1,2,32,128]{3,2,1,0:T(8,128)}, u32[]{:S(2)}) copy-start(f32[1,2,32,128]{3,2,1,0:T(8,128)} %param.14) | copy-start | bytes 98308
  109.0 21.4 %all-to-all-start = ((bf16[1,64,32,128]{3,2,0,1:T(8,128)(2,1)}), bf16[1,64,32,128]{3,2,0,1:T(8,128)(2,1)S(1)}, u32[]{:S(2)}, u32[]{:S(2)}) async-start(bf16[1,64,32,128]{3,2,0,1:T(8,128)(2,1)} %get-tuple-element.48), calls=%async_computation | async-start | bytes 1048576 | tf_op jit(solution)/shard_map/all_to_all | solution.py:87
  131.2 79.5 %copy-start.7 = (f32[1,2,32,128]{3,2,1,0:T(8,128)}, f32[1,2,32,128]{3,2,1,0:T(8,128)S(1)}, u32[]{:S(2)}) copy-start(f32[1,2,32,128]{3,2,1,0:T(8,128)S(1)} %get-tuple-element.39) | copy-start | bytes 98308
  131.2 79.5 %copy-start.8 = (f32[1,2,32,128]{3,2,1,0:T(8,128)}, f32[1,2,32,128]{3,2,1,0:T(8,128)S(1)}, u32[]{:S(2)}) copy-start(f32[1,2,32,128]{3,2,1,0:T(8,128)S(1)} %get-tuple-element.40) | copy-start | bytes 98308
  170.8 24.5 %all-to-all-start.3 = ((bf16[32,1,2,32,128]{4,3,2,1,0:T(8,128)(2,1)}), bf16[32,1,2,32,128]{4,3,2,1,0:T(8,128)(2,1)S(1)}, u32[]{:S(2)}, u32[]{:S(2)}) async-start(bf16[32,1,2,32,128]{4,3,2,1,0:T(8,128)(2,1)} %broadcast_in_dim.50), calls=%async_computation.3 | async-start | bytes 1048576 | tf_op jit(solution)/shard_map/all_to_all | solution.py:36
  195.2 1.0 copy-start.3
  196.2 23.2 %all-to-all-start.1 = ((bf16[32,1,2,32,128]{4,3,2,1,0:T(8,128)(2,1)}), bf16[32,1,2,32,128]{4,3,2,1,0:T(8,128)(2,1)}, u32[]{:S(2)}, u32[]{:S(2)}) async-start(bf16[32,1,2,32,128]{4,3,2,1,0:T(8,128)(2,1)} %broadcast_in_dim.47), calls=%async_computation.1 | async-start | bytes 1048576 | tf_op jit(solution)/shard_map/all_to_all | solution.py:36
  213.7 4.4 %copy-start.9 = (s32[1,64]{1,0:T(1,128)S(1)}, s32[1,64]{1,0:T(1,128)}, u32[]{:S(2)}) copy-start(s32[1,64]{1,0:T(1,128)} %param.13) | copy-start | bytes 772
  213.7 5.0 %copy-start.4 = (bf16[32,1,2,32,128]{4,3,2,1,0:T(8,128)(2,1)S(1)}, bf16[32,1,2,32,128]{4,3,2,1,0:T(8,128)(2,1)}, u32[]{:S(2)}) copy-start(bf16[32,1,2,32,128]{4,3,2,1,0:T(8,128)(2,1)} %copy-done.3) | copy-start | bytes 1572868
  223.4 9.3 %copy-start.1 = (f32[128,8192]{0,1:T(8,128)S(1)}, f32[128,8192]{0,1:T(8,128)}, u32[]{:S(2)}) copy-start(f32[128,8192]{0,1:T(8,128)} %copy.35) | copy-start | bytes 12582916
where the time goes:
time: 248 us; the launch traced here: 243 us
  blocking collectives  68.6 us (28%)
  matrix products  62.1 us (25%)
  local copies, waits for them, and re-layouts  45 us (18%)
  waiting for transfers between devices  31.1 us (13%)
  starting transfers between devices  17.7 us (7%)
  other arithmetic  16.3 us (7%)
  between operations  2.51 us (1%)
    psum x5, blocking collectives, one_axis_at_a_time(): return functools.reduce(lax.psum, axes, shard)  37.9 us
    dot_general x4, matrix products, inverse(): return jnp.einsum('rjpa,rjpb->rajb', picked, right_part, precision=highest)  33.1 us
    all_to_all x1, blocking collectives, per_device(): lax.all_to_all(slot_band.astype(jnp.bfloat16), WIDE, split_axis=1, concat...  30.7 us
    dot_general x2, matrix products, per_device(): jnp.einsum('rjpa,rajb->rjpb', picked, blended, precision=highest)  19.4 us
    all_to_all x1, waiting for transfers between devices, per_device(): lax.all_to_all(slot_band.astype(jnp.bfloat16), WIDE, split_axis=1, concat...  17.1 us
    all_to_all x2, waiting for transfers between devices, from_everyone(): lax.all_to_all(jnp.broadcast_to(shard[None], (length, *shard.shape)), axi...  14 us
    all_to_all x2, starting transfers between devices, from_everyone(): lax.all_to_all(jnp.broadcast_to(shard[None], (length, *shard.shape)), axi...  13.4 us
    unnamed x25, local copies, waits for them, and re-layouts  11.9 us
  transfers between devices with their start and end apart: 3, of which 2 were waited for; matrix products, arithmetic and copies ran while one was open for 8% of the time, Pallas kernels for 0%

commit v1 on v0

v1 whole, which is shorter than its diff:
```python
import functools

import jax
import jax.numpy as jnp
import numpy as np
from jax import lax
from jax.experimental import pallas as pl
from jax.experimental.pallas import tpu as pltpu
from jax.sharding import Mesh
from jax.sharding import PartitionSpec as P

STEPS = 2
BLOCK = 128
BAND = 32
CHUNKS = 8
WIDE = ("zh", "y", "c")
SHARD = ("zl", "x")
MESH = pl.DeviceIdType.MESH
F32 = jnp.float32
BF16 = jnp.bfloat16

momentum_decay = 0.9
beta_one = 0.8
beta_two = 0.95
adam_eps = 1e-08
rms_eps = 1e-06
learning_rate = 0.2


def dct_table(length):
    k = np.arange(length, dtype=np.float64)[:, None]
    n = np.arange(length, dtype=np.float64)[None, :]
    table = np.cos(np.pi * (2.0 * n + 1.0) * k / (2.0 * length))
    return (table * np.where(k == 0.0, np.sqrt(1.0 / length), np.sqrt(2.0 / length))).astype(np.float32)


def split(value):
    high = value.astype(BF16)
    return high, (value - high.astype(F32)).astype(BF16)


def tall(table):
    high = table.astype(BF16)
    low = (table - high.astype(np.float32)).astype(BF16)
    return np.concatenate([high, high, low], axis=0)


def wide_lhs(value):
    high, low = split(value)
    return jnp.concatenate([high, low, high], axis=-1)


def dot(a, b):
    return jnp.dot(a, b, preferred_element_type=F32)


def project_back(rows, coefs):
    p_high, p_low = split(rows)
    q_high, q_low = split(coefs)
    left = jnp.concatenate([p_high, p_low, p_high], axis=0)
    right = jnp.concatenate([q_high, q_high, q_low], axis=0)
    return lax.dot_general(left, right, (((0,), (0,)), ((), ())), preferred_element_type=F32)


def main_kernel(
    offs, order, basis_in, tall_in, mom_in, grad_in, avg_in, sq_in,
    mom_out, gathered, avg_out, sq_out, spread_out,
    mbuf, gbuf, left, band, csend, crecv, ysend, yone, ytwo, zsend, zrecv, own,
    tot_one, tot_two, tot_three, got_one, got_two, got_three,
    load_sem, c_sem, y_sem, z_sem, az_sem, ay_sem, ac_sem, s_sem,
):
    zh, y, c = lax.axis_index("zh"), lax.axis_index("y"), lax.axis_index("c")
    zl, x = lax.axis_index("zl"), lax.axis_index("x")
    n_cb = left.shape[0]
    per = n_cb // CHUNKS
    y_up, y_down = {"y": lax.rem(y + 1, 4)}, {"y": lax.rem(y + 3, 4)}
    other = {"c": 1 - c}

    def zh_at(q):
        return {"zh": lax.rem(zh + q, 4)}

    one_peers = [
        {"zl": lax.rem(zl + i, 2), "x": lax.rem(x + j, 4)} for i in range(2) for j in range(4) if i or j
    ]
    two_peers = [
        {"c": lax.rem(c + i, 2), "y": lax.rem(y + j, 4)} for i in range(2) for j in range(4) if i or j
    ]
    three_peers = [zh_at(q) for q in (1, 2, 3)]

    def load(chunk):
        cols = pl.ds(pl.multiple_of(chunk * (per * BLOCK), 128), per * BLOCK)
        return (
            pltpu.make_async_copy(mom_in.at[0, :, cols], mbuf.at[chunk], load_sem.at[0, chunk]),
            pltpu.make_async_copy(grad_in.at[0, 0, :, cols], gbuf.at[0, chunk], load_sem.at[1, chunk]),
            pltpu.make_async_copy(grad_in.at[1, 0, :, cols], gbuf.at[1, chunk], load_sem.at[2, chunk]),
        )

    def start_load(chunk, _):
        for copy in load(chunk):
            copy.start()
        return 0

    lax.fori_loop(0, CHUNKS, start_load, 0)

    barrier = pltpu.get_barrier_semaphore()
    everyone = one_peers + two_peers + three_peers
    for peer in everyone:
        pl.semaphore_signal(barrier, inc=1, device_id=peer, device_id_type=MESH)

    def bands(chunk, _):
        for copy in load(chunk):
            copy.wait()
        for i in range(per):
            j = chunk * per + i
            cols = slice(i * BLOCK, (i + 1) * BLOCK)
            rows = basis_in[pl.ds(offs[j], BAND), :]
            both = jnp.concatenate(split(rows), axis=0)
            m = dot(both, mbuf[chunk, :, cols])
            g = dot(both, gbuf[0, chunk, :, cols])
            h = dot(both, gbuf[1, chunk, :, cols])
            left[j, 0] = momentum_decay * (m[:BAND] + m[BAND:]) + (g[:BAND] + g[BAND:])
            left[j, 1] = h[:BAND] + h[BAND:]
        value = left[pl.ds(chunk * per, per)].reshape(per * STEPS * BAND, BLOCK)
        out = dot(wide_lhs(value), tall_in[...])
        band[pl.ds(chunk * per, per)] = out.astype(BF16).reshape(per, STEPS, BAND, BLOCK)
        return 0

    lax.fori_loop(0, CHUNKS, bands, 0)

    def slot(r, k, q, core):
        return lax.rem(zh + q, 4) * 16 + lax.rem(y + r, 4) * 4 + core * 2 + k

    def pack(r):
        def body(i, _):
            k, q = i // 4, lax.rem(i, 4)
            csend[r, k, q] = band[order[slot(r, k, q, 1 - c)]]
            return 0

        lax.fori_loop(0, 8, body, 0)

    def remote(src, dst, sems, index, peer):
        return pltpu.make_async_remote_copy(
            src_ref=src, dst_ref=dst, send_sem=sems.at[(0,) + index], recv_sem=sems.at[(1,) + index],
            device_id=peer, device_id_type=MESH,
        )

    sends = []

    def start(copy):
        copy.start()
        sends.append(copy)
        return copy

    ranks = (2, 1, 3, 0)
    c_copies = {}
    pack(2)
    pl.semaphore_wait(barrier, len(everyone))
    for r in ranks:
        if r != 2:
            pack(r)
        c_copies[r] = start(remote(csend.at[r], crecv.at[r], c_sem, (r,), other))

    def merge(r):
        def body(i, _):
            k, q = i // 4, lax.rem(i, 4)
            total = band[order[slot(r, k, q, c)]].astype(F32) + crecv[r, k, q].astype(F32)
            if r == 0:
                own[k, q] = total
            else:
                ysend[r - 1, k, q] = total.astype(BF16)
            return 0

        lax.fori_loop(0, 8, body, 0)

    q_order = (2, 1, 3, 0)
    c_copies[2].wait_recv()
    merge(2)
    first = {}
    for q in q_order:
        first[0, q] = start(remote(ysend.at[1, 0, q], yone.at[0, q], y_sem, (0, q), y_up))
        first[1, q] = start(remote(ysend.at[1, 1, q], yone.at[1, q], y_sem, (1, q), y_down))
    c_copies[1].wait_recv()
    merge(1)
    c_copies[3].wait_recv()
    merge(3)
    early = {}
    for q in q_order:
        early[0, q] = start(remote(ysend.at[0, 1, q], ytwo.at[0, 1, q], y_sem, (2, q), y_up))
        early[1, q] = start(remote(ysend.at[2, 0, q], ytwo.at[1, 0, q], y_sem, (3, q), y_down))
    c_copies[0].wait_recv()
    merge(0)
    late = {}
    for q in q_order:
        first[0, q].wait_recv()
        ysend[0, 0, q] = (ysend[0, 0, q].astype(F32) + yone[0, q].astype(F32)).astype(BF16)
        late[0, q] = start(remote(ysend.at[0, 0, q], ytwo.at[0, 0, q], y_sem, (4, q), y_up))
        first[1, q].wait_recv()
        ysend[2, 1, q] = (ysend[2, 1, q].astype(F32) + yone[1, q].astype(F32)).astype(BF16)
        late[1, q] = start(remote(ysend.at[2, 1, q], ytwo.at[1, 1, q], y_sem, (5, q), y_down))

    def momenta(chunk, _):
        for i in range(per):
            j = chunk * per + i
            cols = slice(i * BLOCK, (i + 1) * BLOCK)
            rows = basis_in[pl.ds(offs[j], BAND), :]
            lost = project_back(rows, momentum_decay * left[j, 0] + left[j, 1])
            blended = momentum_decay * mbuf[chunk, :, cols].astype(F32) + gbuf[0, chunk, :, cols].astype(F32)
            blended = momentum_decay * blended + gbuf[1, chunk, :, cols].astype(F32)
            where = pl.ds(pl.multiple_of(j * BLOCK, 128), BLOCK)
            mom_out[0, :, where] = (blended - lost).astype(BF16)
        return 0

    lax.fori_loop(0, CHUNKS // 2, momenta, 0)

    z_copies = {}
    for q in q_order:
        for copies in (early, late):
            copies[0, q].wait_recv()
            copies[1, q].wait_recv()
        for k in range(2):
            total = own[k, q] + ytwo[0, k, q].astype(F32) + ytwo[1, k, q].astype(F32)
            if q == 0:
                own[k, 0] = total
            else:
                zsend[q - 1, k] = total.astype(BF16)
        if q != 0:
            z_copies[q] = start(remote(zsend.at[q - 1], zrecv.at[q - 1], z_sem, (q - 1,), zh_at(q)))

    lax.fori_loop(CHUNKS // 2, CHUNKS, momenta, 0)

    for q in (1, 3, 2):
        z_copies[q].wait_recv()
    base = zh * 16 + y * 4 + c * 2
    tot_one[...] = jnp.zeros_like(tot_one)
    replicas = lax.axis_size("zh") * lax.axis_size("y") * lax.axis_size("c")
    for k in range(2):
        mean = own[k, 0] + zrecv[0, k].astype(F32) + zrecv[1, k].astype(F32) + zrecv[2, k].astype(F32)
        mean = mean * (1.0 / replicas)
        avg, sq = avg_in[0, k], sq_in[0, k]
        for step in range(STEPS):
            avg = beta_one * avg + (1.0 - beta_one) * mean[step]
            sq = beta_two * sq + (1.0 - beta_two) * mean[step] * mean[step]
            raw = avg / (jnp.sqrt(sq) + adam_eps)
            gathered[base + k, step] = raw.astype(BF16)
            tot_one[step] += jnp.sum((raw * raw).reshape(BAND // 8, 8, BLOCK), axis=0)
        avg_out[0, k] = avg
        sq_out[0, k] = sq

    def block(q, r, core):
        return lax.rem(zh + q, 4) * 16 + lax.rem(y + r, 4) * 4 + core * 2

    mine = gathered.at[pl.ds(base, 2)]
    for q in (2, 1, 3):
        start(remote(mine, mine, az_sem, (q - 1,), zh_at(q)))
    for i, peer in enumerate(one_peers):
        start(remote(tot_one, got_one.at[i], s_sem, (i,), peer))

    def arrived(view, sems, index, peer):
        remote(view, view, sems, index, peer).wait_recv()

    def to_partner(view, index):
        start(remote(view, view, ac_sem, index, other))

    def y_start(q):
        view = gathered.at[pl.ds(block(q, 0, c), 2)]
        start(remote(view, view, ay_sem, (0, q), y_up))
        start(remote(view, view, ay_sem, (1, q), y_down))
        to_partner(view, (0, q))

    def y_forward(q):
        view = gathered.at[pl.ds(block(q, 3, c), 2)]
        arrived(view, ay_sem, (0, q), y_up)
        half = gathered.at[pl.ds(block(q, 3, c), 1)]
        start(remote(half, half, ay_sem, (2, q), y_up))
        to_partner(view, (1, q))
        view = gathered.at[pl.ds(block(q, 1, c), 2)]
        arrived(view, ay_sem, (1, q), y_down)
        half = gathered.at[pl.ds(block(q, 1, c) + 1, 1)]
        start(remote(half, half, ay_sem, (3, q), y_down))
        to_partner(view, (2, q))

    def y_finish(q):
        half = gathered.at[pl.ds(block(q, 2, c), 1)]
        arrived(half, ay_sem, (2, q), y_up)
        to_partner(half, (3, q))
        half = gathered.at[pl.ds(block(q, 2, c) + 1, 1)]
        arrived(half, ay_sem, (3, q), y_down)
        to_partner(half, (4, q))

    def z_arrived(q):
        view = gathered.at[pl.ds(block(q, 0, c), 2)]
        arrived(view, az_sem, (4 - q - 1,), zh_at(q))
        y_start(q)

    y_start(0)
    z_arrived(1)
    z_arrived(3)
    for i, peer in enumerate(one_peers):
        arrived(got_one.at[i], s_sem, (i,), peer)
    tot_two[...] = tot_one[...] + jnp.sum(got_one[...], axis=0)
    for i, peer in enumerate(two_peers):
        start(remote(tot_two, got_two.at[i], s_sem, (7 + i,), peer))
    y_forward(0)
    z_arrived(2)
    y_forward(1)
    y_forward(3)
    for i, peer in enumerate(two_peers):
        arrived(got_two.at[i], s_sem, (7 + i,), peer)
    tot_three[...] = tot_two[...] + jnp.sum(got_two[...], axis=0)
    for i, peer in enumerate(three_peers):
        start(remote(tot_three, got_three.at[i], s_sem, (14 + i,), peer))
    y_finish(0)
    y_forward(2)
    y_finish(1)
    y_finish(3)
    y_finish(2)
    for i, peer in enumerate(three_peers):
        arrived(got_three.at[i], s_sem, (14 + i,), peer)
    spread_out[...] = tot_three[...] + jnp.sum(got_three[...], axis=0)
    for q in range(4):
        there = gathered.at[pl.ds(block(q, 0, 1 - c), 2)]
        arrived(there, ac_sem, (0, q), other)
        there = gathered.at[pl.ds(block(q, 3, 1 - c), 2)]
        arrived(there, ac_sem, (1, q), other)
        there = gathered.at[pl.ds(block(q, 1, 1 - c), 2)]
        arrived(there, ac_sem, (2, q), other)
        there = gathered.at[pl.ds(block(q, 2, 1 - c), 1)]
        arrived(there, ac_sem, (3, q), other)
        there = gathered.at[pl.ds(block(q, 2, 1 - c) + 1, 1)]
        arrived(there, ac_sem, (4, q), other)
    for copy in sends:
        copy.wait_send()


def weight_kernel(
    count, offs, owners, basis_in, tall_in, gathered, sums, avg_in, sq_in, mom_in, w_in,
    w_out, mom_out, avg_out, sq_out, scales, inverse,
):
    step = pl.program_id(0)
    n_slots = gathered.shape[0]
    per = n_slots // CHUNKS

    @pl.when(step == 0)
    def _():
        spreads = []
        for s in range(STEPS):
            total = jnp.sum(sums[s], axis=(0, 1), keepdims=True)
            spread = jnp.sqrt(total * (1.0 / count) + rms_eps)
            scales[s] = jnp.sum(spread)
            spreads.append(spread)

        def body(i, _):
            part = gathered[pl.ds(i * per, per)]
            value = part[:, 0].astype(F32) / spreads[0][None] + part[:, 1].astype(F32) / spreads[1][None]
            out = dot(wide_lhs(value.reshape(per * BAND, BLOCK)), tall_in[...])
            inverse[pl.ds(i * per, per)] = out.reshape(per, BAND, BLOCK)
            return 0

        lax.fori_loop(0, CHUNKS, body, 0)
        avg_out[...] = avg_in[...]
        sq_out[...] = sq_in[...]

    mom_out[...] = mom_in[...]
    for i in range(per):
        j = step * per + i
        cols = slice(i * BLOCK, (i + 1) * BLOCK)
        rows = basis_in[pl.ds(offs[j], BAND), :]
        change = project_back(rows, inverse[owners[j]])
        w_out[:, cols] = (w_in[:, cols].astype(F32) - learning_rate * change).astype(BF16)


def per_device(weights, momentum, grads, offsets, owners, exp_avg, exp_sq):
    n_cb = offsets.shape[1]
    rows, cols = weights.shape
    table = dct_table(BLOCK)
    basis = jnp.asarray(table)
    offs, own = offsets[0], owners[0]
    index = jnp.arange(n_cb, dtype=jnp.int32)
    order = jnp.sum(jnp.where(own[:, None] == index[None, :], index[:, None], 0), axis=0)
    vmem, smem, hbm = (
        pl.BlockSpec(memory_space=s) for s in (pltpu.VMEM, pltpu.SMEM, pl.ANY)
    )
    piece = (STEPS, BAND, BLOCK)
    like = jax.ShapeDtypeStruct
    mom, gathered, avg, sq, sums = pl.pallas_call(
        main_kernel,
        out_shape=(
            like(momentum.shape, BF16),
            like((n_cb,) + piece, BF16),
            like(exp_avg.shape, F32),
            like(exp_sq.shape, F32),
            like((STEPS, 8, BLOCK), F32),
        ),
        in_specs=[smem, smem, vmem, vmem, hbm, hbm, vmem, vmem],
        out_specs=(vmem,) * 5,
        scratch_shapes=[
            pltpu.VMEM((CHUNKS, rows, cols // CHUNKS), BF16),
            pltpu.VMEM((STEPS, CHUNKS, rows, cols // CHUNKS), BF16),
            pltpu.VMEM((n_cb,) + piece, F32),
            pltpu.VMEM((n_cb,) + piece, BF16),
            pltpu.VMEM((4, 2, 4) + piece, BF16),
            pltpu.VMEM((4, 2, 4) + piece, BF16),
            pltpu.VMEM((3, 2, 4) + piece, BF16),
            pltpu.VMEM((2, 4) + piece, BF16),
            pltpu.VMEM((2, 2, 4) + piece, BF16),
            pltpu.VMEM((3, 2) + piece, BF16),
            pltpu.VMEM((3, 2) + piece, BF16),
            pltpu.VMEM((2, 4) + piece, F32),
            pltpu.VMEM((STEPS, 8, BLOCK), F32),
            pltpu.VMEM((STEPS, 8, BLOCK), F32),
            pltpu.VMEM((STEPS, 8, BLOCK), F32),
            pltpu.VMEM((7, STEPS, 8, BLOCK), F32),
            pltpu.VMEM((7, STEPS, 8, BLOCK), F32),
            pltpu.VMEM((3, STEPS, 8, BLOCK), F32),
            pltpu.SemaphoreType.DMA((3, CHUNKS)),
            pltpu.SemaphoreType.DMA((2, 4)),
            pltpu.SemaphoreType.DMA((2, 6, 4)),
            pltpu.SemaphoreType.DMA((2, 3)),
            pltpu.SemaphoreType.DMA((2, 3)),
            pltpu.SemaphoreType.DMA((2, 4, 4)),
            pltpu.SemaphoreType.DMA((2, 5, 4)),
            pltpu.SemaphoreType.DMA((2, 17)),
        ],
        compiler_params=pltpu.CompilerParams(
            collective_id=0, has_side_effects=True, vmem_limit_bytes=40 * 1024 * 1024
        ),
        name="bands",
    )(offs, order, basis, jnp.asarray(tall(table.T)), momentum, grads, exp_avg, exp_sq)

    count = float(exp_avg.size * lax.axis_size(WIDE) * lax.axis_size(SHARD))
    width = cols // CHUNKS
    slab = pl.BlockSpec((rows, width), lambda i: (0, i))
    slab3 = pl.BlockSpec((1, rows, width), lambda i: (0, 0, i))
    new_weights, new_momentum, new_avg, new_sq, scales = pl.pallas_call(
        functools.partial(weight_kernel, count),
        grid=(CHUNKS,),
        out_shape=(
            like(weights.shape, BF16),
            like(momentum.shape, BF16),
            like(exp_avg.shape, F32),
            like(exp_sq.shape, F32),
            like((STEPS,), F32),
        ),
        in_specs=[smem, smem, vmem, vmem, vmem, vmem, vmem, vmem, slab3, slab],
        out_specs=(slab, slab3, vmem, vmem, smem),
        scratch_shapes=[pltpu.VMEM((n_cb, BAND, BLOCK), F32)],
        compiler_params=pltpu.CompilerParams(
            dimension_semantics=("arbitrary",), vmem_limit_bytes=24 * 1024 * 1024
        ),
        name="weights",
    )(offs, own, basis, jnp.asarray(tall(table)), gathered, sums, avg, sq, mom, weights)
    return new_weights, new_momentum, new_avg, new_sq, scales


def solution(mesh):
    split_mesh = Mesh(mesh.devices.reshape(4, 4, 2, 2, 4), ("zh", "y", "c", "zl", "x"))
    in_specs = (
        P(SHARD, None),
        P(WIDE, SHARD, None),
        P(None, WIDE, SHARD, None),
        P(SHARD, None),
        P(SHARD, None),
        P(SHARD, WIDE, None, None),
        P(SHARD, WIDE, None, None),
    )
    out_specs = (
        P(SHARD, None),
        P(WIDE, SHARD, None),
        P(SHARD, WIDE, None, None),
        P(SHARD, WIDE, None, None),
        P(),
    )
    return jax.shard_map(
        per_device, mesh=split_mesh, in_specs=in_specs, out_specs=out_specs, check_vma=False
    )
```

time: 248 us -> 59.9 us (0.24); the launches traced: 243 us -> 59.6 us
  blocking collectives: 68.6 us -> 0 us
  matrix products: 62.1 us -> 0 us
  Pallas kernels: 0 us -> 50.5 us
  local copies, waits for them, and re-layouts: 45 us -> 7.69 us
  waiting for transfers between devices: 31.1 us -> 0 us
  starting transfers between devices: 17.7 us -> 0 us
  other arithmetic: 16.3 us -> 0.75 us
    dot_general x12 -> x0, matrix products: 62.1 us -> none  [the longest x4 33.1 us: inverse(): return jnp.einsum('rjpa,rjpb->rajb', picked, right_part, precision=highest)]
    pallas_call x0 -> x2, Pallas kernels: none -> 50.5 us  [the longest x1 43.5 us: per_device(): pl.pallas_call(main_kernel, out_shape=(like(momentum.shape, BF16), like((...]
    psum x5 -> x0, blocking collectives: 37.9 us -> none  [one_axis_at_a_time(): return functools.reduce(lax.psum, axes, shard)]
    all_to_all x3 -> x0, waiting for transfers between devices: 31.1 us -> none  [the longest x1 17.1 us: per_device(): lax.all_to_all(slot_band.astype(jnp.bfloat16), WIDE, split_axis=1, concat...]
    all_to_all x1 -> x0, blocking collectives: 30.7 us -> none  [per_device(): lax.all_to_all(slot_band.astype(jnp.bfloat16), WIDE, split_axis=1, concat...]
    all_to_all x3 -> x0, starting transfers between devices: 17.7 us -> none  [the longest x2 13.4 us: from_everyone(): lax.all_to_all(jnp.broadcast_to(shard[None], (length, *shard.shape)), axi...]
    convert_element_type x2 -> x0, local copies, waits for them, and re-layouts: 11.2 us -> none  [per_device(): grads[step_index, 0].astype(jnp.float32).reshape(block_shape)]
    gather x5 -> x0, local copies, waits for them, and re-layouts: 10 us -> none  [the longest x1 5.68 us: band_tables(): return basis[indices]]
  transfers between devices with their start and end apart: 3 -> 0, of which waited for: 2 -> 0; matrix products, arithmetic and copies ran while one was open for 8% -> 0% of each run, Pallas kernels for 0% -> 0%
where the time goes in v1:
time: 59.9 us; the launch traced here: 59.6 us
  Pallas kernels  50.5 us (84%)
  local copies, waits for them, and re-layouts  7.69 us (13%)
  other arithmetic  0.75 us (1%)
  between operations  0.68 us (1%)
    pallas_call x1, Pallas kernels, per_device(): pl.pallas_call(main_kernel, out_shape=(like(momentum.shape, BF16), like((...  43.5 us
    unnamed x20, local copies, waits for them, and re-layouts  7.69 us
    pallas_call x1, Pallas kernels, per_device(): pl.pallas_call(functools.partial(weight_kernel, count), grid=(CHUNKS,), o...  6.98 us

profile of v1, /device:TPU:1, one launch (start us, length us, event | category | flops | bytes accessed | tf_op | source)
XLA Modules:
  0.0 59.6 jit_solution(15700298423389495555)
XLA Ops:
  0.6 0.7 %select_reduce_fusion.order = s32[64]{0:T(128)S(1)} fusion(s32[64]{0:T(128)} %bitcast.4), kind=kLoop, calls=%fused_computation | loop fusion | flops 12224 | bytes 512 | tf_op jit(solution)/shard_map/reduce_sum | solution.py:379
  1.4 0.0 copy-start
  1.4 2.2 %copy-done = bf16[2,1,128,8192]{3,2,1,0:T(8,128)(2,1)S(1)} copy-done((bf16[2,1,128,8192]{3,2,1,0:T(8,128)(2,1)S(1)}, bf16[2,1,128,8192]{3,2,1,0:T(8,128)(2,1)}, u32[]{:S(2)}) %copy-start) | copy-done | bytes 4194328
  3.6 0.0 copy-start.1
  3.6 1.6 %copy-done.1 = bf16[1,128,8192]{2,1,0:T(8,128)(2,1)S(1)} copy-done((bf16[1,128,8192]{2,1,0:T(8,128)(2,1)S(1)}, bf16[1,128,8192]{2,1,0:T(8,128)(2,1)}, u32[]{:S(2)}) %copy-start.1) | copy-done | bytes 2097176
  5.2 0.0 copy-start.3
  5.2 0.8 %copy-done.3 = f32[128,128]{1,0:T(8,128)S(1)} copy-done((f32[128,128]{1,0:T(8,128)S(1)}, f32[128,128]{1,0:T(8,128)}, u32[]{:S(2)}) %copy-start.3) | copy-done | bytes 65560
  6.0 0.0 copy-start.5
  6.0 0.9 %copy-done.5 = bf16[384,128]{1,0:T(8,128)(2,1)S(1)} copy-done((bf16[384,128]{1,0:T(8,128)(2,1)S(1)}, bf16[384,128]{1,0:T(8,128)(2,1)}, u32[]{:S(2)}) %copy-start.5) | copy-done | bytes 98328
  6.9 0.0 copy-start.6
  6.9 0.8 %copy-done.6 = f32[1,2,32,128]{3,2,1,0:T(8,128)S(1)} copy-done((f32[1,2,32,128]{3,2,1,0:T(8,128)S(1)}, f32[1,2,32,128]{3,2,1,0:T(8,128)}, u32[]{:S(2)}) %copy-start.6) | copy-done | bytes 32792
  7.7 0.0 copy-start.7
  7.7 0.8 %copy-done.7 = f32[1,2,32,128]{3,2,1,0:T(8,128)S(1)} copy-done((f32[1,2,32,128]{3,2,1,0:T(8,128)S(1)}, f32[1,2,32,128]{3,2,1,0:T(8,128)}, u32[]{:S(2)}) %copy-start.7) | copy-done | bytes 32792
  8.4 0.0 copy-start.8
  8.4 0.7 %copy-done.8 = s32[1,64]{1,0:T(1,128)S(1)} copy-done((s32[1,64]{1,0:T(1,128)S(1)}, s32[1,64]{1,0:T(1,128)}, u32[]{:S(2)}) %copy-start.8) | copy-done | bytes 280
  9.1 0.0 copy-start.2
  9.1 0.0 copy-start.4
  9.1 0.0 copy-start.9
  9.1 43.5 %bands.1 = (bf16[1,128,8192]{2,1,0:T(8,128)(2,1)S(1)}, bf16[64,2,32,128]{3,2,1,0:T(8,128)(2,1)S(1)}, f32[1,2,32,128]{3,2,1,0:T(8,128)S(1)}, f32[1,2,32,128]{3,2,1,0:T(8,128)S(1)}, f32[2,8,128]{2,1,0:T(8,128)S(1)}) custom-call(s32[64]{0:T(128)S(1)} %bitcast.2, s32[64]{0:T(128)S(1)} %select_reduce_fusion.order, f32[128,128]{1,0:T(8,128)S(1)} %copy-done.3, ...), custom_call_target="tpu_custom_call" | custom-call | tf_op jit(solution)/shard_map/bands/pallas_call | solution.py:385
  52.6 0.0 copy-done.2
  52.6 0.0 copy-done.4
  52.6 0.0 copy-done.9
  52.6 7.0 %weights.1 = (bf16[128,8192]{1,0:T(8,128)(2,1)}, bf16[1,128,8192]{2,1,0:T(8,128)(2,1)}, f32[1,2,32,128]{3,2,1,0:T(8,128)}, f32[1,2,32,128]{3,2,1,0:T(8,128)}, f32[2]{0:T(128)}) custom-call(s32[64]{0:T(128)S(1)} %bitcast.3, s32[64]{0:T(128)S(1)} %bitcast.5, f32[128,128]{1,0:T(8,128)S(1)} %copy-done.3, bf16[384,128]{1,0:T(8,128)(2,1)S(1)} %copy-done.4, ...), custom_call_target="tpu_custom_call" | custom-call | tf_op jit(solution)/shard_map/weights/pallas_call | solution.py:434
Async XLA Ops:
  1.4 2.2 %copy-start = (bf16[2,1,128,8192]{3,2,1,0:T(8,128)(2,1)S(1)}, bf16[2,1,128,8192]{3,2,1,0:T(8,128)(2,1)}, u32[]{:S(2)}) copy-start(bf16[2,1,128,8192]{3,2,1,0:T(8,128)(2,1)} %grad_in.1) | copy-start | bytes 12582916
  3.6 1.6 %copy-start.1 = (bf16[1,128,8192]{2,1,0:T(8,128)(2,1)S(1)}, bf16[1,128,8192]{2,1,0:T(8,128)(2,1)}, u32[]{:S(2)}) copy-start(bf16[1,128,8192]{2,1,0:T(8,128)(2,1)} %mom_in.1) | copy-start | bytes 6291460
  5.2 0.8 %copy-start.3 = (f32[128,128]{1,0:T(8,128)S(1)}, f32[128,128]{1,0:T(8,128)}, u32[]{:S(2)}) copy-start(f32[128,128]{1,0:T(8,128)} %constant.8.clone.basis_in) | copy-start | bytes 196612
  6.0 0.9 %copy-start.5 = (bf16[384,128]{1,0:T(8,128)(2,1)S(1)}, bf16[384,128]{1,0:T(8,128)(2,1)}, u32[]{:S(2)}) copy-start(bf16[384,128]{1,0:T(8,128)(2,1)} %constant.9.clone.tall_in) | copy-start | bytes 294916
  6.9 0.8 %copy-start.6 = (f32[1,2,32,128]{3,2,1,0:T(8,128)S(1)}, f32[1,2,32,128]{3,2,1,0:T(8,128)}, u32[]{:S(2)}) copy-start(f32[1,2,32,128]{3,2,1,0:T(8,128)} %avg_in.1) | copy-start | bytes 98308
  7.7 0.8 %copy-start.7 = (f32[1,2,32,128]{3,2,1,0:T(8,128)S(1)}, f32[1,2,32,128]{3,2,1,0:T(8,128)}, u32[]{:S(2)}) copy-start(f32[1,2,32,128]{3,2,1,0:T(8,128)} %sq_in.1) | copy-start | bytes 98308
  8.4 0.7 %copy-start.8 = (s32[1,64]{1,0:T(1,128)S(1)}, s32[1,64]{1,0:T(1,128)}, u32[]{:S(2)}) copy-start(s32[1,64]{1,0:T(1,128)} %param.13) | copy-start | bytes 772
  9.1 43.5 %copy-start.2 = (bf16[128,8192]{1,0:T(8,128)(2,1)S(1)}, bf16[128,8192]{1,0:T(8,128)(2,1)}, u32[]{:S(2)}) copy-start(bf16[128,8192]{1,0:T(8,128)(2,1)} %w_in.1) | copy-start | bytes 6291460
  9.1 43.5 %copy-start.4 = (bf16[384,128]{1,0:T(8,128)(2,1)S(1)}, bf16[384,128]{1,0:T(8,128)(2,1)}, u32[]{:S(2)}) copy-start(bf16[384,128]{1,0:T(8,128)(2,1)} %constant.10.clone.tall_in) | copy-start | bytes 294916
  9.1 43.5 %copy-start.9 = (s32[1,64]{1,0:T(1,128)S(1)}, s32[1,64]{1,0:T(1,128)}, u32[]{:S(2)}) copy-start(s32[1,64]{1,0:T(1,128)} %param.14) | copy-start | bytes 772

commit v2 on v1

v2 whole, which is shorter than its diff:
```python
import functools

import jax
import jax.numpy as jnp
import numpy as np
from jax import lax
from jax.experimental import pallas as pl
from jax.experimental.pallas import tpu as pltpu
from jax.sharding import Mesh
from jax.sharding import PartitionSpec as P

STEPS = 2
BLOCK = 128
BAND = 32
CHUNKS = 8
WIDE = ("zh", "y", "c")
SHARD = ("zl", "x")
MESH = pl.DeviceIdType.MESH
F32 = jnp.float32
BF16 = jnp.bfloat16

momentum_decay = 0.9
beta_one = 0.8
beta_two = 0.95
adam_eps = 1e-08
rms_eps = 1e-06
learning_rate = 0.2


def dct_table(length):
    k = np.arange(length, dtype=np.float64)[:, None]
    n = np.arange(length, dtype=np.float64)[None, :]
    table = np.cos(np.pi * (2.0 * n + 1.0) * k / (2.0 * length))
    return (table * np.where(k == 0.0, np.sqrt(1.0 / length), np.sqrt(2.0 / length))).astype(np.float32)


def split(value):
    high = value.astype(BF16)
    return high, (value - high.astype(F32)).astype(BF16)


def tall(table):
    high = table.astype(BF16)
    low = (table - high.astype(np.float32)).astype(BF16)
    return np.concatenate([high, high, low], axis=0)


def wide_lhs(value):
    high, low = split(value)
    return jnp.concatenate([high, low, high], axis=-1)


def dot(a, b):
    return jnp.dot(a, b, preferred_element_type=F32)


def four_rows(rows):
    high, low = split(rows)
    return jnp.concatenate([high, low, high, low], axis=0)


def four_coefs(coefs):
    high, low = split(coefs)
    return jnp.concatenate([high, high, low, low], axis=0)


def main_kernel(
    offs_hbm, owners_hbm, basis_hbm, tall_hbm, back_hbm, mom_in, grad_in, avg_hbm, sq_hbm,
    mom_out, gathered, turned, avg_out, sq_out, spread_out,
    offs_vec, order_vec, offs_mem, order_mem, basis_in, tall_in, back_in, avg_in, sq_in,
    mbuf, gbuf, left, band, csend, crecv, ysend, yone, ytwo, zsend, zrecv, own,
    tot_one, tot_two, got_one, got_two,
    small_sem, load_sem, c_sem, y_sem, z_sem, az_sem, ay_sem, ac_sem, s_sem,
):
    zh, y, c = lax.axis_index("zh"), lax.axis_index("y"), lax.axis_index("c")
    zl, x = lax.axis_index("zl"), lax.axis_index("x")
    n_cb = left.shape[0]
    per = n_cb // CHUNKS
    y_up, y_down = {"y": lax.rem(y + 1, 4)}, {"y": lax.rem(y + 3, 4)}
    other = {"c": 1 - c}

    def zh_at(q):
        return {"zh": lax.rem(zh + q, 4)}

    one_peers = [
        {"x": lax.rem(x + i, 4), "y": lax.rem(y + j, 4)} for i in (2, 1, 3, 0) for j in (2, 1, 3, 0) if i or j
    ]
    two_peers = [
        {"c": lax.rem(c + i, 2), "zh": lax.rem(zh + q, 4), "zl": lax.rem(zl + j, 2)}
        for q in (2, 1, 3, 0) for j in range(2) for i in range(2) if q or i or j
    ]

    def load(chunk):
        cols = pl.ds(pl.multiple_of(chunk * (per * BLOCK), 128), per * BLOCK)
        return (
            pltpu.make_async_copy(mom_in.at[0, :, cols], mbuf.at[chunk], load_sem.at[0, chunk]),
            pltpu.make_async_copy(grad_in.at[0, 0, :, cols], gbuf.at[0, chunk], load_sem.at[1, chunk]),
            pltpu.make_async_copy(grad_in.at[1, 0, :, cols], gbuf.at[1, chunk], load_sem.at[2, chunk]),
        )

    def start_load(chunk, _):
        for copy in load(chunk):
            copy.start()
        return 0

    small = [
        pltpu.make_async_copy(src, dst, small_sem.at[i])
        for i, (src, dst) in enumerate(
            [
                (owners_hbm, offs_vec),
                (offs_hbm, offs_mem),
                (basis_hbm, basis_in),
                (tall_hbm, tall_in),
                (avg_hbm, avg_in),
                (sq_hbm, sq_in),
                (back_hbm, back_in),
            ]
        )
    ]
    for copy in small[:4]:
        copy.start()
    lax.fori_loop(0, CHUNKS, start_load, 0)
    for copy in small[4:]:
        copy.start()

    barrier = pltpu.get_barrier_semaphore()
    everyone = one_peers + two_peers
    for peer in everyone:
        pl.semaphore_signal(barrier, inc=1, device_id=peer, device_id_type=MESH)

    small[0].wait()
    owner = jnp.concatenate([offs_vec[...], jnp.full((1, BLOCK - n_cb), BLOCK, jnp.int32)], axis=1)
    owner = jnp.transpose(jnp.broadcast_to(owner, (BLOCK, BLOCK)))
    lane = lax.broadcasted_iota(jnp.int32, (BLOCK, BLOCK), 1)
    row = lax.broadcasted_iota(jnp.int32, (BLOCK, BLOCK), 0)
    order_vec[...] = jnp.max(jnp.where(owner == lane, row, 0), axis=0, keepdims=True)
    to_order = pltpu.make_async_copy(order_vec, order_mem, small_sem.at[7])
    to_order.start()
    for copy in small[1:4]:
        copy.wait()

    def bands(chunk, _):
        for copy in load(chunk):
            copy.wait()
        for i in range(per):
            j = chunk * per + i
            cols = slice(i * BLOCK, (i + 1) * BLOCK)
            rows = basis_in[pl.ds(offs_mem[0, j], BAND), :]
            both = jnp.concatenate(split(rows), axis=0)
            m = dot(both, mbuf[chunk, :, cols])
            g = dot(both, gbuf[0, chunk, :, cols])
            h = dot(both, gbuf[1, chunk, :, cols])
            left[j, 0] = momentum_decay * (m[:BAND] + m[BAND:]) + (g[:BAND] + g[BAND:])
            left[j, 1] = h[:BAND] + h[BAND:]
        value = left[pl.ds(chunk * per, per)].reshape(per * STEPS * BAND, BLOCK)
        out = dot(wide_lhs(value), tall_in[...])
        band[pl.ds(chunk * per, per)] = out.astype(BF16).reshape(per, STEPS, BAND, BLOCK)
        return 0

    lax.fori_loop(0, CHUNKS, bands, 0)
    to_order.wait()

    def slot(r, k, q, core):
        return lax.rem(zh + q, 4) * 16 + lax.rem(y + r, 4) * 4 + core * 2 + k

    def pack(r):
        def body(i, _):
            k, q = i // 4, lax.rem(i, 4)
            csend[r, k, q] = band[order_mem[0, slot(r, k, q, 1 - c)]]
            return 0

        lax.fori_loop(0, 8, body, 0)

    def remote(src, dst, sems, index, peer):
        return pltpu.make_async_remote_copy(
            src_ref=src, dst_ref=dst, send_sem=sems.at[(0,) + index], recv_sem=sems.at[(1,) + index],
            device_id=peer, device_id_type=MESH,
        )

    sends = []

    def start(copy):
        copy.start()
        sends.append(copy)
        return copy

    ranks = (2, 1, 3, 0)
    c_copies = {}
    pack(2)
    pl.semaphore_wait(barrier, len(everyone))
    for r in ranks:
        if r != 2:
            pack(r)
        c_copies[r] = start(remote(csend.at[r], crecv.at[r], c_sem, (r,), other))

    def merge(r):
        def body(i, _):
            k, q = i // 4, lax.rem(i, 4)
            total = band[order_mem[0, slot(r, k, q, c)]].astype(F32) + crecv[r, k, q].astype(F32)
            if r == 0:
                own[k, q] = total
            else:
                ysend[r - 1, k, q] = total.astype(BF16)
            return 0

        lax.fori_loop(0, 8, body, 0)

    q_order = (2, 1, 3, 0)
    c_copies[2].wait_recv()
    merge(2)
    first, early, late = {}, {}, {}
    for q in q_order:
        first[0, q] = start(remote(ysend.at[1, 0, q], yone.at[0, q], y_sem, (0, q), y_up))
        first[1, q] = start(remote(ysend.at[1, 1, q], yone.at[1, q], y_sem, (1, q), y_down))
    c_copies[1].wait_recv()
    merge(1)
    c_copies[3].wait_recv()
    merge(3)

    def start_early(q):
        early[0, q] = start(remote(ysend.at[0, 1, q], ytwo.at[0, 1, q], y_sem, (2, q), y_up))
        early[1, q] = start(remote(ysend.at[2, 0, q], ytwo.at[1, 0, q], y_sem, (3, q), y_down))

    def start_late(q):
        first[0, q].wait_recv()
        ysend[0, 0, q] = (ysend[0, 0, q].astype(F32) + yone[0, q].astype(F32)).astype(BF16)
        late[0, q] = start(remote(ysend.at[0, 0, q], ytwo.at[0, 0, q], y_sem, (4, q), y_up))
        first[1, q].wait_recv()
        ysend[2, 1, q] = (ysend[2, 1, q].astype(F32) + yone[1, q].astype(F32)).astype(BF16)
        late[1, q] = start(remote(ysend.at[2, 1, q], ytwo.at[1, 1, q], y_sem, (5, q), y_down))

    start_early(2)
    start_early(1)
    c_copies[0].wait_recv()
    merge(0)
    start_late(2)
    start_early(3)
    start_late(1)
    start_early(0)
    start_late(3)
    start_late(0)

    def momenta(chunk, _):
        for i in range(per):
            j = chunk * per + i
            cols = slice(i * BLOCK, (i + 1) * BLOCK)
            back = jnp.transpose(four_rows(basis_in[pl.ds(offs_mem[0, j], BAND), :]))
            turned[j] = back
            lost = dot(back, four_coefs(momentum_decay * left[j, 0] + left[j, 1]))
            blended = momentum_decay * mbuf[chunk, :, cols].astype(F32) + gbuf[0, chunk, :, cols].astype(F32)
            blended = momentum_decay * blended + gbuf[1, chunk, :, cols].astype(F32)
            where = pl.ds(pl.multiple_of(j * BLOCK, 128), BLOCK)
            mom_out[0, :, where] = (blended - lost).astype(BF16)
        return 0

    lax.fori_loop(0, CHUNKS // 2, momenta, 0)

    z_copies = {}
    for q in q_order:
        for copies in (early, late):
            copies[0, q].wait_recv()
            copies[1, q].wait_recv()
        for k in range(2):
            total = own[k, q] + ytwo[0, k, q].astype(F32) + ytwo[1, k, q].astype(F32)
            if q == 0:
                own[k, 0] = total
            else:
                zsend[q - 1, k] = total.astype(BF16)
        if q != 0:
            z_copies[q] = start(remote(zsend.at[q - 1], zrecv.at[q - 1], z_sem, (q - 1,), zh_at(q)))

    lax.fori_loop(CHUNKS // 2, CHUNKS, momenta, 0)

    for q in (1, 3, 2):
        z_copies[q].wait_recv()
    for copy in small[4:]:
        copy.wait()
    base = zh * 16 + y * 4 + c * 2
    replicas = lax.axis_size("zh") * lax.axis_size("y") * lax.axis_size("c")
    raws = []
    sums = [jnp.zeros((1, BLOCK), F32)] * STEPS
    for k in range(2):
        mean = own[k, 0] + zrecv[0, k].astype(F32) + zrecv[1, k].astype(F32) + zrecv[2, k].astype(F32)
        mean = mean * (1.0 / replicas)
        avg, sq = avg_in[0, k], sq_in[0, k]
        for step in range(STEPS):
            avg = beta_one * avg + (1.0 - beta_one) * mean[step]
            sq = beta_two * sq + (1.0 - beta_two) * mean[step] * mean[step]
            raw = avg / (jnp.sqrt(sq) + adam_eps)
            sums[step] += jnp.sum(raw * raw, axis=0, keepdims=True)
            raws.append(raw)
        avg_out[0, k] = avg
        sq_out[0, k] = sq
    spatial = dot(wide_lhs(jnp.concatenate(raws, axis=0)), back_in[...])
    gathered[pl.ds(base, 2)] = spatial.astype(BF16).reshape(2, STEPS, BAND, BLOCK)
    tot_one[...] = jnp.concatenate(sums, axis=0)

    def one(q, r, core, k):
        return gathered.at[lax.rem(zh + q, 4) * 16 + lax.rem(y + r, 4) * 4 + core * 2 + k]

    def share(view, sems, index, peer):
        start(remote(view, view, sems, index, peer))

    def arrived(view, sems, index, peer):
        remote(view, view, sems, index, peer).wait_recv()

    for q in (2, 1, 3):
        for k in range(2):
            share(one(0, 0, c, k), az_sem, (q - 1, k), zh_at(q))

    def y_start(q):
        for k in range(2):
            share(one(q, 0, c, k), ay_sem, (0, q, k), y_up)
            share(one(q, 0, c, 1 - k), ay_sem, (1, q, 1 - k), y_down)
        for k in range(2):
            share(one(q, 0, c, k), ac_sem, (0, q, k), other)

    def y_forward(q):
        arrived(one(q, 3, c, 0), ay_sem, (0, q, 0), y_up)
        share(one(q, 3, c, 0), ay_sem, (2, q, 0), y_up)
        share(one(q, 3, c, 0), ac_sem, (3, q, 0), other)
        arrived(one(q, 1, c, 1), ay_sem, (1, q, 1), y_down)
        share(one(q, 1, c, 1), ay_sem, (2, q, 1), y_down)
        share(one(q, 1, c, 1), ac_sem, (1, q, 1), other)
        arrived(one(q, 3, c, 1), ay_sem, (0, q, 1), y_up)
        share(one(q, 3, c, 1), ac_sem, (3, q, 1), other)
        arrived(one(q, 1, c, 0), ay_sem, (1, q, 0), y_down)
        share(one(q, 1, c, 0), ac_sem, (1, q, 0), other)

    def y_finish(q):
        arrived(one(q, 2, c, 0), ay_sem, (2, q, 0), y_up)
        share(one(q, 2, c, 0), ac_sem, (2, q, 0), other)
        arrived(one(q, 2, c, 1), ay_sem, (2, q, 1), y_down)
        share(one(q, 2, c, 1), ac_sem, (2, q, 1), other)

    def z_arrived(q):
        for k in range(2):
            arrived(one(q, 0, c, k), az_sem, (4 - q - 1, k), zh_at(q))
        y_start(q)

    y_start(0)
    for i, peer in enumerate(one_peers):
        start(remote(tot_one, got_one.at[i], s_sem, (i,), peer))
    y_forward(0)
    z_arrived(1)
    z_arrived(3)
    total = tot_one[...]
    for i, peer in enumerate(one_peers):
        arrived(got_one.at[i], s_sem, (i,), peer)
        total += got_one[i]
    tot_two[...] = total
    for i, peer in enumerate(two_peers):
        start(remote(tot_two, got_two.at[i], s_sem, (15 + i,), peer))
    z_arrived(2)
    y_finish(0)
    y_forward(1)
    y_forward(3)
    y_forward(2)
    y_finish(1)
    y_finish(3)
    y_finish(2)
    for i, peer in enumerate(two_peers):
        arrived(got_two.at[i], s_sem, (15 + i,), peer)
        total += got_two[i]
    spread_out[...] = total
    for q in range(4):
        for r in range(4):
            for k in range(2):
                arrived(one(q, r, 1 - c, k), ac_sem, (r, q, k), other)
    for copy in sends:
        copy.wait_send()


def weight_kernel(
    count, owners, gathered, turned, sums, avg_in, sq_in, mom_in, w_in,
    w_out, mom_out, avg_out, sq_out, scales, buffer, out_sem, same_sem,
):
    n_slots = gathered.shape[0]
    per = n_slots // CHUNKS
    same = [
        pltpu.make_async_copy(src, dst, same_sem.at[i])
        for i, (src, dst) in enumerate([(mom_in, mom_out), (avg_in, avg_out), (sq_in, sq_out)])
    ]
    for copy in same:
        copy.start()
    parts = []
    for s in range(STEPS):
        total = jnp.sum(sums[s : s + 1], axis=1, keepdims=True)
        spread = jnp.sqrt(total * (1.0 / count) + rms_eps)
        scales[s] = jnp.sum(spread)
        parts.append(-learning_rate / spread)

    def store(chunk):
        cols = pl.ds(pl.multiple_of(chunk * (per * BLOCK), 128), per * BLOCK)
        return pltpu.make_async_copy(buffer.at[:, cols], w_out.at[:, cols], out_sem.at[chunk])

    def body(chunk, _):
        for i in range(per):
            j = chunk * per + i
            pair = gathered[owners[0, j]]
            change = dot(turned[j], four_coefs(pair[0].astype(F32) * parts[0] + pair[1].astype(F32) * parts[1]))
            cols = pl.ds(pl.multiple_of(j * BLOCK, 128), BLOCK)
            buffer[:, cols] = (w_in[:, cols].astype(F32) + change).astype(BF16)
        store(chunk).start()
        return 0

    lax.fori_loop(0, CHUNKS, body, 0)

    def drain(chunk, _):
        store(chunk).wait()
        return 0

    lax.fori_loop(0, CHUNKS, drain, 0)
    for copy in same:
        copy.wait()


def per_device(weights, momentum, grads, offsets, owners, exp_avg, exp_sq):
    n_cb = offsets.shape[1]
    rows, cols = weights.shape
    table = dct_table(BLOCK)
    basis = jnp.asarray(table)
    vmem, smem, hbm = (
        pl.BlockSpec(memory_space=s) for s in (pltpu.VMEM, pltpu.SMEM, pltpu.HBM)
    )
    piece = (STEPS, BAND, BLOCK)
    like = jax.ShapeDtypeStruct
    mom, gathered, turned, avg, sq, sums = pl.pallas_call(
        main_kernel,
        out_shape=(
            like(momentum.shape, BF16),
            like((n_cb,) + piece, BF16),
            like((n_cb, BLOCK, BLOCK), BF16),
            like(exp_avg.shape, F32),
            like(exp_sq.shape, F32),
            like((STEPS, BLOCK), F32),
        ),
        in_specs=[hbm] * 9,
        out_specs=(vmem,) * 6,
        scratch_shapes=[
            pltpu.VMEM((1, n_cb), jnp.int32),
            pltpu.VMEM((1, BLOCK), jnp.int32),
            pltpu.SMEM((1, n_cb), jnp.int32),
            pltpu.SMEM((1, BLOCK), jnp.int32),
            pltpu.VMEM((BLOCK, BLOCK), F32),
            pltpu.VMEM((3 * BLOCK, BLOCK), BF16),
            pltpu.VMEM((3 * BLOCK, BLOCK), BF16),
            pltpu.VMEM(exp_avg.shape, F32),
            pltpu.VMEM(exp_sq.shape, F32),
            pltpu.VMEM((CHUNKS, rows, cols // CHUNKS), BF16),
            pltpu.VMEM((STEPS, CHUNKS, rows, cols // CHUNKS), BF16),
            pltpu.VMEM((n_cb,) + piece, F32),
            pltpu.VMEM((n_cb,) + piece, BF16),
            pltpu.VMEM((4, 2, 4) + piece, BF16),
            pltpu.VMEM((4, 2, 4) + piece, BF16),
            pltpu.VMEM((3, 2, 4) + piece, BF16),
            pltpu.VMEM((2, 4) + piece, BF16),
            pltpu.VMEM((2, 2, 4) + piece, BF16),
            pltpu.VMEM((3, 2) + piece, BF16),
            pltpu.VMEM((3, 2) + piece, BF16),
            pltpu.VMEM((2, 4) + piece, F32),
            pltpu.VMEM((STEPS, BLOCK), F32),
            pltpu.VMEM((STEPS, BLOCK), F32),
            pltpu.VMEM((15, STEPS, BLOCK), F32),
            pltpu.VMEM((15, STEPS, BLOCK), F32),
            pltpu.SemaphoreType.DMA((8,)),
            pltpu.SemaphoreType.DMA((3, CHUNKS)),
            pltpu.SemaphoreType.DMA((2, 4)),
            pltpu.SemaphoreType.DMA((2, 6, 4)),
            pltpu.SemaphoreType.DMA((2, 3)),
            pltpu.SemaphoreType.DMA((2, 3, 2)),
            pltpu.SemaphoreType.DMA((2, 3, 4, 2)),
            pltpu.SemaphoreType.DMA((2, 4, 4, 2)),
            pltpu.SemaphoreType.DMA((2, 30)),
        ],
        compiler_params=pltpu.CompilerParams(
            collective_id=0, has_side_effects=True, vmem_limit_bytes=40 * 1024 * 1024
        ),
        name="bands",
    )(
        *(
            pltpu.with_memory_space_constraint(array, pltpu.HBM)
            for array in (
                offsets, owners, basis, jnp.asarray(tall(table.T)), jnp.asarray(tall(table)), momentum, grads, exp_avg, exp_sq
            )
        )
    )

    count = float(exp_avg.size * lax.axis_size(WIDE) * lax.axis_size(SHARD))
    anywhere = pl.BlockSpec(memory_space=pl.ANY)
    new_weights, new_momentum, new_avg, new_sq, scales = pl.pallas_call(
        functools.partial(weight_kernel, count),
        out_shape=(
            like(weights.shape, BF16),
            like(momentum.shape, BF16),
            like(exp_avg.shape, F32),
            like(exp_sq.shape, F32),
            like((STEPS,), F32),
        ),
        in_specs=[smem] + [vmem] * 7,
        out_specs=(anywhere,) * 4 + (smem,),
        scratch_shapes=[
            pltpu.VMEM(weights.shape, BF16),
            pltpu.SemaphoreType.DMA((CHUNKS,)),
            pltpu.SemaphoreType.DMA((3,)),
        ],
        compiler_params=pltpu.CompilerParams(vmem_limit_bytes=24 * 1024 * 1024),
        name="weights",
    )(owners, gathered, turned, sums, avg, sq, mom, weights)
    return new_weights, new_momentum, new_avg, new_sq, scales


def solution(mesh):
    split_mesh = Mesh(mesh.devices.reshape(4, 4, 2, 2, 4), ("zh", "y", "c", "zl", "x"))
    in_specs = (
        P(SHARD, None),
        P(WIDE, SHARD, None),
        P(None, WIDE, SHARD, None),
        P(SHARD, None),
        P(SHARD, None),
        P(SHARD, WIDE, None, None),
        P(SHARD, WIDE, None, None),
    )
    out_specs = (
        P(SHARD, None),
        P(WIDE, SHARD, None),
        P(SHARD, WIDE, None, None),
        P(SHARD, WIDE, None, None),
        P(),
    )
    return jax.shard_map(
        per_device, mesh=split_mesh, in_specs=in_specs, out_specs=out_specs, check_vma=False
    )
```

time: 59.9 us -> 46.1 us (0.77)
  local copies, waits for them, and re-layouts: 7.69 us -> 0.01 us
  Pallas kernels: 50.5 us -> 45.4 us
  other arithmetic: 0.75 us -> 0 us
    unnamed x20 -> x4, local copies, waits for them, and re-layouts: 7.69 us -> 0.01 us
    pallas_call x1, Pallas kernels: 6.98 us -> 3.95 us  [per_device(): pl.pallas_call(functools.partial(weight_kernel, count), out_shape=(like(w...]
    pallas_call x1, Pallas kernels: 43.5 us -> 41.5 us  [per_device(): pl.pallas_call(main_kernel, out_shape=(like(momentum.shape, BF16), like((...]
    reduce_sum x1 -> x0, other arithmetic: 0.75 us -> none  [per_device(): jnp.sum(jnp.where(own[:, None] == index[None, :], index[:, None], 0), axi...]
where the time goes in v2:
time: 46.1 us
  Pallas kernels  45.4 us (98%)
  between operations  0.67 us (1%)
    pallas_call x1, Pallas kernels, per_device(): pl.pallas_call(main_kernel, out_shape=(like(momentum.shape, BF16), like((...  41.5 us
    pallas_call x1, Pallas kernels, per_device(): pl.pallas_call(functools.partial(weight_kernel, count), out_shape=(like(w...  3.95 us

profile of v2, /device:TPU:1, one launch (start us, length us, event | category | flops | bytes accessed | tf_op | source)
XLA Modules:
  0.0 46.1 jit_solution(1287488241198564944)
XLA Ops:
  0.6 0.0 copy-start.1
  0.6 0.0 copy-start
  0.7 41.5 %bands.1 = (bf16[1,128,8192]{2,1,0:T(8,128)(2,1)S(1)}, bf16[64,2,32,128]{3,2,1,0:T(8,128)(2,1)S(1)}, bf16[64,128,128]{2,1,0:T(8,128)(2,1)S(1)}, f32[1,2,32,128]{...) custom-call(s32[1,64]{1,0:T(1,128)} %offs_hbm.1, s32[1,64]{1,0:T(1,128)} %owners.1, ...), custom_call_target="tpu_custom_call" | custom-call | tf_op jit(solution)/shard_map/bands/pallas_call | solution.py:428
  42.1 0.0 copy-done.1
  42.1 0.0 copy-done
  42.1 3.9 %weights.1 = (bf16[128,8192]{1,0:T(8,128)(2,1)}, bf16[1,128,8192]{2,1,0:T(8,128)(2,1)}, f32[1,2,32,128]{3,2,1,0:T(8,128)}, f32[1,2,32,128]{3,2,1,0:T(8,128)}, f32[2]{0:T(128)}) custom-call(s32[1,64]{1,0:T(1,128)S(1)} %copy-done.1, bf16[64,2,32,128]{3,2,1,0:T(8,128)(2,1)S(1)} %get-tuple-element.11.gathered, ...), custom_call_target="tpu_custom_call" | custom-call | tf_op jit(solution)/shard_map/weights/pallas_call | solution.py:491
Async XLA Ops:
  0.6 41.5 %copy-start.1 = (s32[1,64]{1,0:T(1,128)S(1)}, s32[1,64]{1,0:T(1,128)}, u32[]{:S(2)}) copy-start(s32[1,64]{1,0:T(1,128)} %owners.1) | copy-start | bytes 772
  0.6 41.5 %copy-start = (bf16[128,8192]{1,0:T(8,128)(2,1)S(1)}, bf16[128,8192]{1,0:T(8,128)(2,1)}, u32[]{:S(2)}) copy-start(bf16[128,8192]{1,0:T(8,128)(2,1)} %w_in.1) | copy-start | bytes 6291460
